TPU v7x, 32 devices: a whole 2x2x4 slice. The times are simulated.
32 devices in a mesh: sky: 4 (over x, core), tm: 8 (over z, y).
Axes of the slice: x: 2, y: 2, z: 4, core: 2. Of those that a mesh axis runs over, the one named last changes fastest.
Arguments:
- attitude: float32 [4, 8, 512], P(None, 'tm', 'sky'), may hold values from -6 to 6
- slot_time: float32 [262144], P(('sky', 'tm')), may hold values from -1 to 1
- slot_parallax: float32 [262144], P(('sky', 'tm')), may hold values from -1 to 1
- slot_observed: float32 [262144], P(('sky', 'tm')), may hold values from -6 to 6
- slot_phase: float32 [262144], P(('sky', 'tm')), may hold values from 0 to 1
- slot_knot: int32 [262144], P(('sky', 'tm')), may hold values from 0 to 508
- block_source: int32 [8192], P(('sky', 'tm')), may hold values from 0 to 63
- block_count: int32 [8192], P(('sky', 'tm')), may hold values from 1 to 32
- prior: float32 [5, 256], P(None, ('sky', 'tm')), may hold values from 0.5 to 4
Outputs:
- update: float32 [5, 256], P(None, ('sky', 'tm'))
Inputs may be any that keep to these rules, and one draw needn't show every extreme that they name: The four knots from slot_knot on lie in the transit's time group of 512 knots. `block_source`: an index into the 64 sources of the block's own sky sector.
All inputs are finite; a program needn't handle non-finite values.
Results may differ from a plain program's by a relative error of at most 0.0003.
Values sent between devices are 32-bit elements; how exact they have to be, the bound alone decides.
A program may use at most 64 MiB of HBM per device.

v0:
```python
import math
import jax
import jax.numpy as jnp
from jax import lax
from jax.sharding import PartitionSpec as P

PAIR_LIST = [(i, j) for i in range(5) for j in range(i, 5)]


def spline_quat(table, knot, phase):
    total = knot.shape[0]
    width = table.shape[1]
    step = math.gcd(total, 512)
    knot_rows = knot.reshape(total // step, step)
    phase_rows = phase.reshape(total // step, step)
    positions = jnp.arange(width, dtype=jnp.int32)

    def one_block(items):
        knot_here, phase_here = items
        weights = [
            (1.0 - phase_here) ** 3 / 6.0,
            (3.0 * phase_here**3 - 6.0 * phase_here**2 + 4.0) / 6.0,
            (-3.0 * phase_here**3 + 3.0 * phase_here**2 + 3.0 * phase_here + 1.0) / 6.0,
            phase_here**3 / 6.0,
        ]
        offset = positions[None, :] - knot_here[:, None]
        spread = jnp.zeros((step, width), jnp.float32)
        for i in range(4):
            spread = jnp.where(offset == i, weights[i][:, None], spread)
        return lax.dot_general(
            table,
            spread,
            (((1,), (1,)), ((), ())),
            precision=lax.Precision.HIGHEST,
            preferred_element_type=jnp.float32,
        )

    quat = lax.map(one_block, (knot_rows, phase_rows))
    return jnp.transpose(quat, (1, 0, 2)).reshape(4, total)


def block_sums(table, knot, phase, time, parallax, observed, count):
    quat = spline_quat(table, knot, phase)
    cross = quat[0] * quat[0] + quat[1] * quat[1] - quat[2] * quat[2] - quat[3] * quat[3]
    along = 2.0 * (quat[1] * quat[2] + quat[0] * quat[3])
    tilt = 2.0 * (quat[1] * quat[3] - quat[0] * quat[2])
    design = [cross, along, parallax, time * cross, time * along]
    residual = observed - tilt
    rows = [design[i] * design[j] for i, j in PAIR_LIST] + [design[i] * residual for i in range(5)]
    stacked = jnp.stack(rows)
    blocks = count.shape[0]
    stacked = stacked.reshape(20, blocks, -1)
    live = (jnp.arange(stacked.shape[2], dtype=jnp.int32)[None, :] < count[:, None]).astype(
        stacked.dtype
    )
    return jnp.sum(stacked * live[None], axis=2)


def source_sums(sums, block_source, sector_sources):
    blocks = block_source.shape[0]
    step = math.gcd(blocks, 512)
    source_rows = block_source.reshape(blocks // step, step)
    sum_rows = jnp.transpose(sums.reshape(20, blocks // step, step), (1, 0, 2))
    positions = jnp.arange(sector_sources, dtype=jnp.int32)

    def add_block(carry, items):
        source_here, sums_here = items
        member = (source_here[:, None] == positions[None, :]).astype(jnp.float32)
        return (
            carry
            + jnp.dot(
                sums_here,
                member,
                precision=lax.Precision.HIGHEST,
                preferred_element_type=jnp.float32,
            ),
            None,
        )

    start = jnp.zeros((20, sector_sources), jnp.float32)
    total, _ = lax.scan(add_block, start, (source_rows, sum_rows))
    return total


def solve_normals(normal, prior):
    entry = {}
    for index, pair in enumerate(PAIR_LIST):
        entry[pair[1], pair[0]] = normal[index]
    for i in range(5):
        entry[i, i] = entry[i, i] + prior[i]
    lower = {}
    for col in range(5):
        pivot = entry[col, col]
        for k in range(col):
            pivot = pivot - lower[col, k] * lower[col, k]
        root = jnp.sqrt(pivot)
        lower[col, col] = root
        for row in range(col + 1, 5):
            value = entry[row, col]
            for k in range(col):
                value = value - lower[row, k] * lower[col, k]
            lower[row, col] = value / root
    forward = []
    for i in range(5):
        value = normal[15 + i]
        for k in range(i):
            value = value - lower[i, k] * forward[k]
        forward.append(value / lower[i, i])
    result = [None] * 5
    for i in range(4, -1, -1):
        value = forward[i]
        for k in range(i + 1, 5):
            value = value - lower[k, i] * result[k]
        result[i] = value / lower[i, i]
    return jnp.stack(result)


def on_device(
    attitude,
    slot_time,
    slot_parallax,
    slot_observed,
    slot_phase,
    slot_knot,
    block_source,
    block_count,
    prior,
):
    group = lax.all_gather(attitude, "sky", axis=2, tiled=True)
    table = group[:, 0, :]
    sums = block_sums(
        table, slot_knot, slot_phase, slot_time, slot_parallax, slot_observed, block_count
    )
    owned = prior.shape[1]
    sector_sources = owned * lax.axis_size("tm")
    partial_value = source_sums(sums, block_source, sector_sources)
    total = lax.psum(partial_value, "tm")
    normal = lax.dynamic_slice_in_dim(total, lax.axis_index("tm") * owned, owned, 1)
    return solve_normals(normal, prior)


def solution(mesh):
    in_specs = (
        P(None, "tm", "sky"),
        P(("sky", "tm")),
        P(("sky", "tm")),
        P(("sky", "tm")),
        P(("sky", "tm")),
        P(("sky", "tm")),
        P(("sky", "tm")),
        P(("sky", "tm")),
        P(None, ("sky", "tm")),
    )
    out_specs = P(None, ("sky", "tm"))
    return jax.shard_map(
        on_device, mesh=mesh, in_specs=in_specs, out_specs=out_specs, check_vma=False
    )
```

profile of v0, /device:TPU:0, one launch (start us, length us, event | category | flops | bytes accessed | tf_op | source)
XLA Modules:
  0.0 77.9 jit_solution(18191354367063263991)
XLA Ops:
  0.0 0.8 reshape.292
  0.8 0.7 copy-done.4
  1.5 6.2 %all_gather.3 = f32[4,1,512]{2,0,1:T(4,128)S(1)} all-gather(f32[4,1,128]{2,0,1:T(4,128)S(1)} %bitcast.33), channel_id=1, replica_groups=mesh['sky'=4,'tm'=8] {'sky'}, dimensions={2}, use_global_device_ids=true | all-gather | bytes 10240 | tf_op jit(solution)/shard_map/all_gather | solution.py:129
  7.6 22.9 %while.3 = (s32[]{:T(128)}, f32[16,4,512]{2,1,0:T(4,128)S(1)}, s32[16,512]{1,0:T(8,128)S(1)}, f32[16,512]{1,0:T(8,128)S(1)}, f32[4,512]{1,0:T(4,128)S(1)}, /*index=5*/s32[]{:T(128)}) while((s32[]{:T(128)}, f32[16,4,512]{2,1,0:T(4,128)S(1)}, s32[16,512]{1,0:T(8,128)S(1)}, f32[16,512]{1,0:T(8,128)S(1)}, f32[4,512]{1,0:T(4,128)S(1)}, ...), condition=%wide.region_1.2_spmd.clone, body=%wide.region_0.1_spmd.clone.sunk | while | flops 14951938 | bytes 45145 | solution.py:38
  7.6 1.4 %fusion.59 = f32[16,4,512]{2,1,0:T(4,128)S(1)} fusion(f32[16,4,512]{2,1,0:T(4,128)S(1)} %get-tuple-element.192, s32[]{:T(128)S(6)} %copy.59, f32[4,512]{1,0:T(4,128)S(1)} %get-tuple-element.201, f32[512]{0:T(512)S(1)} %get-tuple-element.181, f32[512]{0:T(512)S(1)} %get-tuple-element.182, f32[512]{0:T(512)S(1)} %get-tuple-element.183, ...), kind=kOutput, calls=%fused_computation.2.clone.1 | convolution fusion | flops 14942208 | bytes 26628 | tf_op jit(solution)/shard_map/while/body/eval_jaxpr/dot_general | solution.py:30
  9.1 1.4 %fusion.59 = f32[16,4,512]{2,1,0:T(4,128)S(1)} fusion(f32[16,4,512]{2,1,0:T(4,128)S(1)} %get-tuple-element.192, s32[]{:T(128)S(6)} %copy.59, f32[4,512]{1,0:T(4,128)S(1)} %get-tuple-element.201, f32[512]{0:T(512)S(1)} %get-tuple-element.181, f32[512]{0:T(512)S(1)} %get-tuple-element.182, f32[512]{0:T(512)S(1)} %get-tuple-element.183, ...), kind=kOutput, calls=%fused_computation.2.clone.1 | convolution fusion | flops 14942208 | bytes 26628 | tf_op jit(solution)/shard_map/while/body/eval_jaxpr/dot_general | solution.py:30
  10.5 1.4 %fusion.59 = f32[16,4,512]{2,1,0:T(4,128)S(1)} fusion(f32[16,4,512]{2,1,0:T(4,128)S(1)} %get-tuple-element.192, s32[]{:T(128)S(6)} %copy.59, f32[4,512]{1,0:T(4,128)S(1)} %get-tuple-element.201, f32[512]{0:T(512)S(1)} %get-tuple-element.181, f32[512]{0:T(512)S(1)} %get-tuple-element.182, f32[512]{0:T(512)S(1)} %get-tuple-element.183, ...), kind=kOutput, calls=%fused_computation.2.clone.1 | convolution fusion | flops 14942208 | bytes 26628 | tf_op jit(solution)/shard_map/while/body/eval_jaxpr/dot_general | solution.py:30
  12.0 1.4 %fusion.59 = f32[16,4,512]{2,1,0:T(4,128)S(1)} fusion(f32[16,4,512]{2,1,0:T(4,128)S(1)} %get-tuple-element.192, s32[]{:T(128)S(6)} %copy.59, f32[4,512]{1,0:T(4,128)S(1)} %get-tuple-element.201, f32[512]{0:T(512)S(1)} %get-tuple-element.181, f32[512]{0:T(512)S(1)} %get-tuple-element.182, f32[512]{0:T(512)S(1)} %get-tuple-element.183, ...), kind=kOutput, calls=%fused_computation.2.clone.1 | convolution fusion | flops 14942208 | bytes 26628 | tf_op jit(solution)/shard_map/while/body/eval_jaxpr/dot_general | solution.py:30
  13.4 1.4 %fusion.59 = f32[16,4,512]{2,1,0:T(4,128)S(1)} fusion(f32[16,4,512]{2,1,0:T(4,128)S(1)} %get-tuple-element.192, s32[]{:T(128)S(6)} %copy.59, f32[4,512]{1,0:T(4,128)S(1)} %get-tuple-element.201, f32[512]{0:T(512)S(1)} %get-tuple-element.181, f32[512]{0:T(512)S(1)} %get-tuple-element.182, f32[512]{0:T(512)S(1)} %get-tuple-element.183, ...), kind=kOutput, calls=%fused_computation.2.clone.1 | convolution fusion | flops 14942208 | bytes 26628 | tf_op jit(solution)/shard_map/while/body/eval_jaxpr/dot_general | solution.py:30
  14.8 1.4 %fusion.59 = f32[16,4,512]{2,1,0:T(4,128)S(1)} fusion(f32[16,4,512]{2,1,0:T(4,128)S(1)} %get-tuple-element.192, s32[]{:T(128)S(6)} %copy.59, f32[4,512]{1,0:T(4,128)S(1)} %get-tuple-element.201, f32[512]{0:T(512)S(1)} %get-tuple-element.181, f32[512]{0:T(512)S(1)} %get-tuple-element.182, f32[512]{0:T(512)S(1)} %get-tuple-element.183, ...), kind=kOutput, calls=%fused_computation.2.clone.1 | convolution fusion | flops 14942208 | bytes 26628 | tf_op jit(solution)/shard_map/while/body/eval_jaxpr/dot_general | solution.py:30
  16.3 1.4 %fusion.59 = f32[16,4,512]{2,1,0:T(4,128)S(1)} fusion(f32[16,4,512]{2,1,0:T(4,128)S(1)} %get-tuple-element.192, s32[]{:T(128)S(6)} %copy.59, f32[4,512]{1,0:T(4,128)S(1)} %get-tuple-element.201, f32[512]{0:T(512)S(1)} %get-tuple-element.181, f32[512]{0:T(512)S(1)} %get-tuple-element.182, f32[512]{0:T(512)S(1)} %get-tuple-element.183, ...), kind=kOutput, calls=%fused_computation.2.clone.1 | convolution fusion | flops 14942208 | bytes 26628 | tf_op jit(solution)/shard_map/while/body/eval_jaxpr/dot_general | solution.py:30
  17.7 1.4 %fusion.59 = f32[16,4,512]{2,1,0:T(4,128)S(1)} fusion(f32[16,4,512]{2,1,0:T(4,128)S(1)} %get-tuple-element.192, s32[]{:T(128)S(6)} %copy.59, f32[4,512]{1,0:T(4,128)S(1)} %get-tuple-element.201, f32[512]{0:T(512)S(1)} %get-tuple-element.181, f32[512]{0:T(512)S(1)} %get-tuple-element.182, f32[512]{0:T(512)S(1)} %get-tuple-element.183, ...), kind=kOutput, calls=%fused_computation.2.clone.1 | convolution fusion | flops 14942208 | bytes 26628 | tf_op jit(solution)/shard_map/while/body/eval_jaxpr/dot_general | solution.py:30
  19.1 1.4 %fusion.59 = f32[16,4,512]{2,1,0:T(4,128)S(1)} fusion(f32[16,4,512]{2,1,0:T(4,128)S(1)} %get-tuple-element.192, s32[]{:T(128)S(6)} %copy.59, f32[4,512]{1,0:T(4,128)S(1)} %get-tuple-element.201, f32[512]{0:T(512)S(1)} %get-tuple-element.181, f32[512]{0:T(512)S(1)} %get-tuple-element.182, f32[512]{0:T(512)S(1)} %get-tuple-element.183, ...), kind=kOutput, calls=%fused_computation.2.clone.1 | convolution fusion | flops 14942208 | bytes 26628 | tf_op jit(solution)/shard_map/while/body/eval_jaxpr/dot_general | solution.py:30
  20.6 1.4 %fusion.59 = f32[16,4,512]{2,1,0:T(4,128)S(1)} fusion(f32[16,4,512]{2,1,0:T(4,128)S(1)} %get-tuple-element.192, s32[]{:T(128)S(6)} %copy.59, f32[4,512]{1,0:T(4,128)S(1)} %get-tuple-element.201, f32[512]{0:T(512)S(1)} %get-tuple-element.181, f32[512]{0:T(512)S(1)} %get-tuple-element.182, f32[512]{0:T(512)S(1)} %get-tuple-element.183, ...), kind=kOutput, calls=%fused_computation.2.clone.1 | convolution fusion | flops 14942208 | bytes 26628 | tf_op jit(solution)/shard_map/while/body/eval_jaxpr/dot_general | solution.py:30
  22.0 1.4 %fusion.59 = f32[16,4,512]{2,1,0:T(4,128)S(1)} fusion(f32[16,4,512]{2,1,0:T(4,128)S(1)} %get-tuple-element.192, s32[]{:T(128)S(6)} %copy.59, f32[4,512]{1,0:T(4,128)S(1)} %get-tuple-element.201, f32[512]{0:T(512)S(1)} %get-tuple-element.181, f32[512]{0:T(512)S(1)} %get-tuple-element.182, f32[512]{0:T(512)S(1)} %get-tuple-element.183, ...), kind=kOutput, calls=%fused_computation.2.clone.1 | convolution fusion | flops 14942208 | bytes 26628 | tf_op jit(solution)/shard_map/while/body/eval_jaxpr/dot_general | solution.py:30
  23.4 1.4 %fusion.59 = f32[16,4,512]{2,1,0:T(4,128)S(1)} fusion(f32[16,4,512]{2,1,0:T(4,128)S(1)} %get-tuple-element.192, s32[]{:T(128)S(6)} %copy.59, f32[4,512]{1,0:T(4,128)S(1)} %get-tuple-element.201, f32[512]{0:T(512)S(1)} %get-tuple-element.181, f32[512]{0:T(512)S(1)} %get-tuple-element.182, f32[512]{0:T(512)S(1)} %get-tuple-element.183, ...), kind=kOutput, calls=%fused_computation.2.clone.1 | convolution fusion | flops 14942208 | bytes 26628 | tf_op jit(solution)/shard_map/while/body/eval_jaxpr/dot_general | solution.py:30
  24.9 1.4 %fusion.59 = f32[16,4,512]{2,1,0:T(4,128)S(1)} fusion(f32[16,4,512]{2,1,0:T(4,128)S(1)} %get-tuple-element.192, s32[]{:T(128)S(6)} %copy.59, f32[4,512]{1,0:T(4,128)S(1)} %get-tuple-element.201, f32[512]{0:T(512)S(1)} %get-tuple-element.181, f32[512]{0:T(512)S(1)} %get-tuple-element.182, f32[512]{0:T(512)S(1)} %get-tuple-element.183, ...), kind=kOutput, calls=%fused_computation.2.clone.1 | convolution fusion | flops 14942208 | bytes 26628 | tf_op jit(solution)/shard_map/while/body/eval_jaxpr/dot_general | solution.py:30
  26.3 1.4 %fusion.59 = f32[16,4,512]{2,1,0:T(4,128)S(1)} fusion(f32[16,4,512]{2,1,0:T(4,128)S(1)} %get-tuple-element.192, s32[]{:T(128)S(6)} %copy.59, f32[4,512]{1,0:T(4,128)S(1)} %get-tuple-element.201, f32[512]{0:T(512)S(1)} %get-tuple-element.181, f32[512]{0:T(512)S(1)} %get-tuple-element.182, f32[512]{0:T(512)S(1)} %get-tuple-element.183, ...), kind=kOutput, calls=%fused_computation.2.clone.1 | convolution fusion | flops 14942208 | bytes 26628 | tf_op jit(solution)/shard_map/while/body/eval_jaxpr/dot_general | solution.py:30
  27.7 1.4 %fusion.59 = f32[16,4,512]{2,1,0:T(4,128)S(1)} fusion(f32[16,4,512]{2,1,0:T(4,128)S(1)} %get-tuple-element.192, s32[]{:T(128)S(6)} %copy.59, f32[4,512]{1,0:T(4,128)S(1)} %get-tuple-element.201, f32[512]{0:T(512)S(1)} %get-tuple-element.181, f32[512]{0:T(512)S(1)} %get-tuple-element.182, f32[512]{0:T(512)S(1)} %get-tuple-element.183, ...), kind=kOutput, calls=%fused_computation.2.clone.1 | convolution fusion | flops 14942208 | bytes 26628 | tf_op jit(solution)/shard_map/while/body/eval_jaxpr/dot_general | solution.py:30
  29.2 1.4 %fusion.59 = f32[16,4,512]{2,1,0:T(4,128)S(1)} fusion(f32[16,4,512]{2,1,0:T(4,128)S(1)} %get-tuple-element.192, s32[]{:T(128)S(6)} %copy.59, f32[4,512]{1,0:T(4,128)S(1)} %get-tuple-element.201, f32[512]{0:T(512)S(1)} %get-tuple-element.181, f32[512]{0:T(512)S(1)} %get-tuple-element.182, f32[512]{0:T(512)S(1)} %get-tuple-element.183, ...), kind=kOutput, calls=%fused_computation.2.clone.1 | convolution fusion | flops 14942208 | bytes 26628 | tf_op jit(solution)/shard_map/while/body/eval_jaxpr/dot_general | solution.py:30
  30.5 0.4 multiply_reduce_fusion.1
  31.3 0.7 copy-done
  32.1 0.7 copy-done.1
  36.2 0.7 copy-done.6
  36.9 0.6 copy-done.7
  37.5 0.3 fusion.39
  37.9 37.9 %psum.7 = f32[20,64]{0,1:T(8,128)S(1)} all-reduce(f32[20,64]{0,1:T(8,128)S(1)} %fusion.39), channel_id=1, replica_groups=mesh['sky'=4,'tm'=8] {'tm'}, use_global_device_ids=true, to_apply=%region_3.4 | all-reduce | flops 1280 | bytes 10240 | tf_op jit(solution)/shard_map/psum | solution.py:137
  75.8 0.7 copy-done.5
  76.8 0.1 subtract_divide_fusion.7
  76.9 0.1 subtract_divide_fusion.4
  77.1 0.1 subtract_divide_fusion
  77.3 0.7 copy.50
  (133 shorter events, 4.6 us)
Async XLA Ops:
  0.0 0.8 copy-start.3
  0.8 0.7 copy-start.4
  31.3 0.8 copy-start
  31.3 0.8 %copy-start.2 = (f32[8192]{0:T(1024)S(1)}, f32[8192]{0:T(1024)}, u32[]{:S(2)}) copy-start(f32[8192]{0:T(1024)} %param.14) | copy-start | bytes 98308
  32.1 0.8 copy-start.1
  36.1 0.7 copy-start.6
  36.8 0.7 copy-start.7
  75.8 0.7 copy-start.5
where the time goes:
time: 78.4 us; the launch traced here: 77.9 us
  blocking collectives  44.1 us (56%)
  matrix products  22.3 us (28%)
  local copies, waits for them, and re-layouts  9.75 us (12%)
  other arithmetic  1.07 us (1%)
    psum x1, blocking collectives, on_device(): total = lax.psum(partial_value, 'tm')  37.9 us
    dot_general x16, matrix products, one_block(): lax.dot_general(table, spread, (((1,), (1,)), ((), ())), precision=lax.Pr...  22 us
    all_gather x1, blocking collectives, on_device(): group = lax.all_gather(attitude, 'sky', axis=2, tiled=True)  6.15 us
    unnamed x40, local copies, waits for them, and re-layouts  4.73 us
    another operation x35, local copies, waits for them, and re-layouts, block_sums(): stacked = jnp.stack(rows)  2.6 us

commit v1 on v0

--- a/solution.py
+++ b/solution.py
@@ -134,7 +134,7 @@
     owned = prior.shape[1]
     sector_sources = owned * lax.axis_size("tm")
     partial_value = source_sums(sums, block_source, sector_sources)
-    total = lax.psum(partial_value, "tm")
+    total = jax.lax.all_gather(partial_value, "tm").sum(axis=0)
     normal = lax.dynamic_slice_in_dim(total, lax.axis_index("tm") * owned, owned, 1)
     return solve_normals(normal, prior)
 

time: 78.4 us -> 71.2 us (0.908)
  blocking collectives: 44.1 us -> 37.5 us
    psum x1 -> x0, blocking collectives: 37.9 us -> none  [on_device(): total = lax.psum(partial_value, 'tm')]
    all_gather x0 -> x1, blocking collectives: none -> 31.4 us  [on_device(): total = jax.lax.all_gather(partial_value, 'tm').sum(axis=0)]
    unnamed x40 -> x35, local copies, waits for them, and re-layouts: 4.73 us -> 4.32 us
where the time goes in v1:
time: 71.2 us; the launch traced here: 70.8 us
  blocking collectives  37.5 us (53%)
  matrix products  22.2 us (31%)
  local copies, waits for them, and re-layouts  9.2 us (13%)
  other arithmetic  1.11 us (2%)
    all_gather x1, blocking collectives, on_device(): total = jax.lax.all_gather(partial_value, 'tm').sum(axis=0)  31.4 us
    dot_general x16, matrix products, one_block(): lax.dot_general(table, spread, (((1,), (1,)), ((), ())), precision=lax.Pr...  22 us
    all_gather x1, blocking collectives, on_device(): group = lax.all_gather(attitude, 'sky', axis=2, tiled=True)  6.15 us
    unnamed x35, local copies, waits for them, and re-layouts  4.32 us
    another operation x35, local copies, waits for them, and re-layouts, block_sums(): stacked = jnp.stack(rows)  2.6 us

profile of v1, /device:TPU:0, one launch (start us, length us, event | category | flops | bytes accessed | tf_op | source)
XLA Modules:
  0.0 70.8 jit_solution(6305110734064752692)
XLA Ops:
  0.0 0.8 %reshape.292 = s32[16,512]{1,0:T(8,128)S(1)} reshape(s32[8192]{0:T(1024)} %param.16) | data formatting | bytes 65536 | tf_op jit(solution)/shard_map/reshape | solution.py:14
  0.8 0.7 copy-done.4
  1.5 6.2 %all_gather.9 = f32[4,1,512]{2,0,1:T(4,128)S(1)} all-gather(f32[4,1,128]{2,0,1:T(4,128)S(1)} %bitcast.35), channel_id=1, replica_groups=mesh['sky'=4,'tm'=8] {'sky'}, dimensions={2}, use_global_device_ids=true | all-gather | bytes 10240 | tf_op jit(solution)/shard_map/all_gather | solution.py:129
  7.6 22.9 %while.3 = (s32[]{:T(128)}, f32[16,4,512]{2,1,0:T(4,128)S(1)}, s32[16,512]{1,0:T(8,128)S(1)}, f32[16,512]{1,0:T(8,128)S(1)}, f32[4,512]{1,0:T(4,128)S(1)}, /*index=5*/s32[]{:T(128)}) while((s32[]{:T(128)}, f32[16,4,512]{2,1,0:T(4,128)S(1)}, s32[16,512]{1,0:T(8,128)S(1)}, f32[16,512]{1,0:T(8,128)S(1)}, f32[4,512]{1,0:T(4,128)S(1)}, ...), condition=%wide.region_1.2_spmd.clone, body=%wide.region_0.1_spmd.clone.sunk | while | flops 14951938 | bytes 45145 | solution.py:38
  7.6 1.4 %fusion.93 = f32[16,4,512]{2,1,0:T(4,128)S(1)} fusion(f32[16,4,512]{2,1,0:T(4,128)S(1)} %get-tuple-element.187, s32[]{:T(128)S(6)} %copy.36, f32[4,512]{1,0:T(4,128)S(1)} %get-tuple-element.196, f32[512]{0:T(512)S(1)} %get-tuple-element.176, f32[512]{0:T(512)S(1)} %get-tuple-element.177, f32[512]{0:T(512)S(1)} %get-tuple-element.178, ...), kind=kOutput, calls=%fused_computation.2.clone.1 | convolution fusion | flops 14942208 | bytes 26628 | tf_op jit(solution)/shard_map/while/body/eval_jaxpr/dot_general | solution.py:30
  9.1 1.4 %fusion.93 = f32[16,4,512]{2,1,0:T(4,128)S(1)} fusion(f32[16,4,512]{2,1,0:T(4,128)S(1)} %get-tuple-element.187, s32[]{:T(128)S(6)} %copy.36, f32[4,512]{1,0:T(4,128)S(1)} %get-tuple-element.196, f32[512]{0:T(512)S(1)} %get-tuple-element.176, f32[512]{0:T(512)S(1)} %get-tuple-element.177, f32[512]{0:T(512)S(1)} %get-tuple-element.178, ...), kind=kOutput, calls=%fused_computation.2.clone.1 | convolution fusion | flops 14942208 | bytes 26628 | tf_op jit(solution)/shard_map/while/body/eval_jaxpr/dot_general | solution.py:30
  10.5 1.4 %fusion.93 = f32[16,4,512]{2,1,0:T(4,128)S(1)} fusion(f32[16,4,512]{2,1,0:T(4,128)S(1)} %get-tuple-element.187, s32[]{:T(128)S(6)} %copy.36, f32[4,512]{1,0:T(4,128)S(1)} %get-tuple-element.196, f32[512]{0:T(512)S(1)} %get-tuple-element.176, f32[512]{0:T(512)S(1)} %get-tuple-element.177, f32[512]{0:T(512)S(1)} %get-tuple-element.178, ...), kind=kOutput, calls=%fused_computation.2.clone.1 | convolution fusion | flops 14942208 | bytes 26628 | tf_op jit(solution)/shard_map/while/body/eval_jaxpr/dot_general | solution.py:30
  12.0 1.4 %fusion.93 = f32[16,4,512]{2,1,0:T(4,128)S(1)} fusion(f32[16,4,512]{2,1,0:T(4,128)S(1)} %get-tuple-element.187, s32[]{:T(128)S(6)} %copy.36, f32[4,512]{1,0:T(4,128)S(1)} %get-tuple-element.196, f32[512]{0:T(512)S(1)} %get-tuple-element.176, f32[512]{0:T(512)S(1)} %get-tuple-element.177, f32[512]{0:T(512)S(1)} %get-tuple-element.178, ...), kind=kOutput, calls=%fused_computation.2.clone.1 | convolution fusion | flops 14942208 | bytes 26628 | tf_op jit(solution)/shard_map/while/body/eval_jaxpr/dot_general | solution.py:30
  13.4 1.4 %fusion.93 = f32[16,4,512]{2,1,0:T(4,128)S(1)} fusion(f32[16,4,512]{2,1,0:T(4,128)S(1)} %get-tuple-element.187, s32[]{:T(128)S(6)} %copy.36, f32[4,512]{1,0:T(4,128)S(1)} %get-tuple-element.196, f32[512]{0:T(512)S(1)} %get-tuple-element.176, f32[512]{0:T(512)S(1)} %get-tuple-element.177, f32[512]{0:T(512)S(1)} %get-tuple-element.178, ...), kind=kOutput, calls=%fused_computation.2.clone.1 | convolution fusion | flops 14942208 | bytes 26628 | tf_op jit(solution)/shard_map/while/body/eval_jaxpr/dot_general | solution.py:30
  14.8 1.4 %fusion.93 = f32[16,4,512]{2,1,0:T(4,128)S(1)} fusion(f32[16,4,512]{2,1,0:T(4,128)S(1)} %get-tuple-element.187, s32[]{:T(128)S(6)} %copy.36, f32[4,512]{1,0:T(4,128)S(1)} %get-tuple-element.196, f32[512]{0:T(512)S(1)} %get-tuple-element.176, f32[512]{0:T(512)S(1)} %get-tuple-element.177, f32[512]{0:T(512)S(1)} %get-tuple-element.178, ...), kind=kOutput, calls=%fused_computation.2.clone.1 | convolution fusion | flops 14942208 | bytes 26628 | tf_op jit(solution)/shard_map/while/body/eval_jaxpr/dot_general | solution.py:30
  16.3 1.4 %fusion.93 = f32[16,4,512]{2,1,0:T(4,128)S(1)} fusion(f32[16,4,512]{2,1,0:T(4,128)S(1)} %get-tuple-element.187, s32[]{:T(128)S(6)} %copy.36, f32[4,512]{1,0:T(4,128)S(1)} %get-tuple-element.196, f32[512]{0:T(512)S(1)} %get-tuple-element.176, f32[512]{0:T(512)S(1)} %get-tuple-element.177, f32[512]{0:T(512)S(1)} %get-tuple-element.178, ...), kind=kOutput, calls=%fused_computation.2.clone.1 | convolution fusion | flops 14942208 | bytes 26628 | tf_op jit(solution)/shard_map/while/body/eval_jaxpr/dot_general | solution.py:30
  17.7 1.4 %fusion.93 = f32[16,4,512]{2,1,0:T(4,128)S(1)} fusion(f32[16,4,512]{2,1,0:T(4,128)S(1)} %get-tuple-element.187, s32[]{:T(128)S(6)} %copy.36, f32[4,512]{1,0:T(4,128)S(1)} %get-tuple-element.196, f32[512]{0:T(512)S(1)} %get-tuple-element.176, f32[512]{0:T(512)S(1)} %get-tuple-element.177, f32[512]{0:T(512)S(1)} %get-tuple-element.178, ...), kind=kOutput, calls=%fused_computation.2.clone.1 | convolution fusion | flops 14942208 | bytes 26628 | tf_op jit(solution)/shard_map/while/body/eval_jaxpr/dot_general | solution.py:30
  19.1 1.4 %fusion.93 = f32[16,4,512]{2,1,0:T(4,128)S(1)} fusion(f32[16,4,512]{2,1,0:T(4,128)S(1)} %get-tuple-element.187, s32[]{:T(128)S(6)} %copy.36, f32[4,512]{1,0:T(4,128)S(1)} %get-tuple-element.196, f32[512]{0:T(512)S(1)} %get-tuple-element.176, f32[512]{0:T(512)S(1)} %get-tuple-element.177, f32[512]{0:T(512)S(1)} %get-tuple-element.178, ...), kind=kOutput, calls=%fused_computation.2.clone.1 | convolution fusion | flops 14942208 | bytes 26628 | tf_op jit(solution)/shard_map/while/body/eval_jaxpr/dot_general | solution.py:30
  20.6 1.4 %fusion.93 = f32[16,4,512]{2,1,0:T(4,128)S(1)} fusion(f32[16,4,512]{2,1,0:T(4,128)S(1)} %get-tuple-element.187, s32[]{:T(128)S(6)} %copy.36, f32[4,512]{1,0:T(4,128)S(1)} %get-tuple-element.196, f32[512]{0:T(512)S(1)} %get-tuple-element.176, f32[512]{0:T(512)S(1)} %get-tuple-element.177, f32[512]{0:T(512)S(1)} %get-tuple-element.178, ...), kind=kOutput, calls=%fused_computation.2.clone.1 | convolution fusion | flops 14942208 | bytes 26628 | tf_op jit(solution)/shard_map/while/body/eval_jaxpr/dot_general | solution.py:30
  22.0 1.4 %fusion.93 = f32[16,4,512]{2,1,0:T(4,128)S(1)} fusion(f32[16,4,512]{2,1,0:T(4,128)S(1)} %get-tuple-element.187, s32[]{:T(128)S(6)} %copy.36, f32[4,512]{1,0:T(4,128)S(1)} %get-tuple-element.196, f32[512]{0:T(512)S(1)} %get-tuple-element.176, f32[512]{0:T(512)S(1)} %get-tuple-element.177, f32[512]{0:T(512)S(1)} %get-tuple-element.178, ...), kind=kOutput, calls=%fused_computation.2.clone.1 | convolution fusion | flops 14942208 | bytes 26628 | tf_op jit(solution)/shard_map/while/body/eval_jaxpr/dot_general | solution.py:30
  23.4 1.4 %fusion.93 = f32[16,4,512]{2,1,0:T(4,128)S(1)} fusion(f32[16,4,512]{2,1,0:T(4,128)S(1)} %get-tuple-element.187, s32[]{:T(128)S(6)} %copy.36, f32[4,512]{1,0:T(4,128)S(1)} %get-tuple-element.196, f32[512]{0:T(512)S(1)} %get-tuple-element.176, f32[512]{0:T(512)S(1)} %get-tuple-element.177, f32[512]{0:T(512)S(1)} %get-tuple-element.178, ...), kind=kOutput, calls=%fused_computation.2.clone.1 | convolution fusion | flops 14942208 | bytes 26628 | tf_op jit(solution)/shard_map/while/body/eval_jaxpr/dot_general | solution.py:30
  24.9 1.4 %fusion.93 = f32[16,4,512]{2,1,0:T(4,128)S(1)} fusion(f32[16,4,512]{2,1,0:T(4,128)S(1)} %get-tuple-element.187, s32[]{:T(128)S(6)} %copy.36, f32[4,512]{1,0:T(4,128)S(1)} %get-tuple-element.196, f32[512]{0:T(512)S(1)} %get-tuple-element.176, f32[512]{0:T(512)S(1)} %get-tuple-element.177, f32[512]{0:T(512)S(1)} %get-tuple-element.178, ...), kind=kOutput, calls=%fused_computation.2.clone.1 | convolution fusion | flops 14942208 | bytes 26628 | tf_op jit(solution)/shard_map/while/body/eval_jaxpr/dot_general | solution.py:30
  26.3 1.4 %fusion.93 = f32[16,4,512]{2,1,0:T(4,128)S(1)} fusion(f32[16,4,512]{2,1,0:T(4,128)S(1)} %get-tuple-element.187, s32[]{:T(128)S(6)} %copy.36, f32[4,512]{1,0:T(4,128)S(1)} %get-tuple-element.196, f32[512]{0:T(512)S(1)} %get-tuple-element.176, f32[512]{0:T(512)S(1)} %get-tuple-element.177, f32[512]{0:T(512)S(1)} %get-tuple-element.178, ...), kind=kOutput, calls=%fused_computation.2.clone.1 | convolution fusion | flops 14942208 | bytes 26628 | tf_op jit(solution)/shard_map/while/body/eval_jaxpr/dot_general | solution.py:30
  27.7 1.4 %fusion.93 = f32[16,4,512]{2,1,0:T(4,128)S(1)} fusion(f32[16,4,512]{2,1,0:T(4,128)S(1)} %get-tuple-element.187, s32[]{:T(128)S(6)} %copy.36, f32[4,512]{1,0:T(4,128)S(1)} %get-tuple-element.196, f32[512]{0:T(512)S(1)} %get-tuple-element.176, f32[512]{0:T(512)S(1)} %get-tuple-element.177, f32[512]{0:T(512)S(1)} %get-tuple-element.178, ...), kind=kOutput, calls=%fused_computation.2.clone.1 | convolution fusion | flops 14942208 | bytes 26628 | tf_op jit(solution)/shard_map/while/body/eval_jaxpr/dot_general | solution.py:30
  29.2 1.4 %fusion.93 = f32[16,4,512]{2,1,0:T(4,128)S(1)} fusion(f32[16,4,512]{2,1,0:T(4,128)S(1)} %get-tuple-element.187, s32[]{:T(128)S(6)} %copy.36, f32[4,512]{1,0:T(4,128)S(1)} %get-tuple-element.196, f32[512]{0:T(512)S(1)} %get-tuple-element.176, f32[512]{0:T(512)S(1)} %get-tuple-element.177, f32[512]{0:T(512)S(1)} %get-tuple-element.178, ...), kind=kOutput, calls=%fused_computation.2.clone.1 | convolution fusion | flops 14942208 | bytes 26628 | tf_op jit(solution)/shard_map/while/body/eval_jaxpr/dot_general | solution.py:30
  30.5 0.4 multiply_reduce_fusion.1
  31.3 0.7 %copy-done = f32[8192]{0:T(1024)S(1)} copy-done((f32[8192]{0:T(1024)S(1)}, f32[8192]{0:T(1024)}, u32[]{:S(2)}) %copy-start) | copy-done | bytes 32792
  32.1 0.7 %copy-done.1 = f32[8192]{0:T(1024)S(1)} copy-done((f32[8192]{0:T(1024)S(1)}, f32[8192]{0:T(1024)}, u32[]{:S(2)}) %copy-start.1) | copy-done | bytes 32792
  36.2 0.7 copy-done.6
  36.9 0.6 copy-done.7
  37.5 0.2 convolution_bitcast_fusion.1
  37.8 31.4 %all-gather.1 = f32[8,20,64]{2,1,0:T(8,128)S(1)} all-gather(f32[1,20,64]{2,1,0:T(8,128)S(1)} %convolution_bitcast_fusion.1), channel_id=2, replica_groups=mesh['sky'=4,'tm'=8] {'tm'}, dimensions={0}, use_global_device_ids=true | all-gather | bytes 46080 | tf_op jit(solution)/shard_map/all_gather | solution.py:137
  69.2 0.7 copy-done.5
  69.9 0.1 fusion.66
  70.0 0.1 fusion.67
  70.1 0.1 subtract_divide_fusion
  70.2 0.6 stack.83
  (126 shorter events, 4.1 us)
Async XLA Ops:
  0.0 0.8 %copy-start.3 = (f32[8192]{0:T(1024)S(1)}, f32[8192]{0:T(1024)}, u32[]{:S(2)}) copy-start(f32[8192]{0:T(1024)} %param.15) | copy-start | bytes 98308
  0.8 0.7 copy-start.4
  31.3 0.8 %copy-start = (f32[8192]{0:T(1024)S(1)}, f32[8192]{0:T(1024)}, u32[]{:S(2)}) copy-start(f32[8192]{0:T(1024)} %param.12) | copy-start | bytes 98308
  31.3 0.8 %copy-start.2 = (f32[8192]{0:T(1024)S(1)}, f32[8192]{0:T(1024)}, u32[]{:S(2)}) copy-start(f32[8192]{0:T(1024)} %param.14) | copy-start | bytes 98308
  32.1 0.8 %copy-start.1 = (f32[8192]{0:T(1024)S(1)}, f32[8192]{0:T(1024)}, u32[]{:S(2)}) copy-start(f32[8192]{0:T(1024)} %param.13) | copy-start | bytes 98308
  36.1 0.7 copy-start.6
  36.8 0.7 copy-start.7
  69.2 0.7 copy-start.5
